TPU v7x, 512 devices: a whole 4x4x16 slice. The times are simulated.
512 devices in a mesh: ka: 128 (over y, x_hi, z), col: 4 (over x_lo, core).
Axes of the slice: x: 4 (x_hi: 2, x_lo: 2; x = x_hi * 2 + x_lo), y: 4, z: 16, core: 2. Of those that a mesh axis runs over, the one named last changes fastest.
Arguments:
- amps: bfloat16 [256, 256, 192], P('ka', 'col'), may hold values from -6 to 6
- isdf_coeffs: bfloat16 [256, 2048, 256], P('ka', 'col'), may hold values from -0.375 to 0.375
- w_screen: bfloat16 [16, 2048, 2048], P(None, 'ka', 'col'), as said below
- energies: float32 [256, 256], P('ka', 'col'), may hold values from 0.5 to 3
- qsel: int32 [2], replicated, may hold values from 0 to 15
- partner: int32 [2, 256], replicated, may hold values from 0 to 255, each once within a row
Outputs:
- applied: float32 [256, 256, 192], P('ka', 'col')
Inputs may be any that keep to these rules, and one draw needn't show every extreme that they name: Each row of partner is a permutation of the 256 k points. `w_screen`: each of the 16 matrices is symmetric.
All inputs are finite; a program needn't handle non-finite values.
Results may differ from a plain program's by a relative error of at most 0.013.
Values may be sent and summed in bfloat16 or wider, within the bound.
No kernel may reach another device: no remote copies, remote signals or barrier semaphores. Data moves between devices by JAX's collectives and lax.ppermute only.
A program may use at most 64 MiB of HBM per device.

v0:
```python
import jax
import jax.numpy as jnp
from jax import lax
from jax.sharding import Mesh
from jax.sharding import PartitionSpec as P

KA = ("ka_0", "ka_1", "ka_2")


def laid_out(pieces, dim):
    lengths = list(pieces.shape[1:])
    lengths[dim] *= pieces.shape[0]
    return jnp.moveaxis(pieces, 0, dim).reshape(lengths)


def gather_in_order(array, axes, order):
    pieces = array[None]
    for k in order:
        pieces = lax.all_gather(pieces, axes[k], axis=0, tiled=True)
    carried = [lax.axis_size(axes[k]) for k in reversed(order)]
    pieces = pieces.reshape(*carried, *array.shape)
    turned = sorted(range(len(order)), key=lambda place: order[len(order) - 1 - place])
    return pieces.transpose(*turned, *range(len(order), pieces.ndim)).reshape(-1, *array.shape)


def gather_axes(array, axes, order, dim):
    return laid_out(gather_in_order(array, axes, order), dim)


def sent_to_all(array, axis):
    length = lax.axis_size(axis)
    return lax.all_to_all(
        jnp.broadcast_to(array[None], (length, *array.shape)), axis, 0, 0, tiled=True
    )


def collect(array, axis, dim):
    pieces = sent_to_all(array, axis)
    return laid_out(pieces, dim)


def split_up(array, dim, length):
    before, after = (array.shape[:dim], array.shape[dim + 1 :])
    return jnp.moveaxis(array.reshape(*before, length, -1, *after), dim, 0)


def sent_and_summed(array, axis, dim):
    pieces = split_up(array, dim, lax.axis_size(axis))
    arrived = lax.all_to_all(pieces, axis, split_axis=0, concat_axis=0, tiled=True)
    return arrived.astype(jnp.float32).sum(axis=0)


def body(amps, isdf_coeffs, w_screen, energies, qsel, partner):
    k_local = amps.shape[0]
    vectors = amps.shape[2]
    offset_base = lax.axis_index(KA) * k_local
    owned = offset_base + jnp.arange(k_local, dtype=jnp.int32)
    wanted = jnp.take(partner, owned, axis=1).reshape(-1)
    everyone = gather_axes(amps, KA, (1, 0, 2), 0)
    picked = jnp.take(everyone, wanted, axis=0)
    partners = collect(picked, "col", 1)
    partners = partners.reshape(2, k_local, partners.shape[1], vectors)
    densities = jnp.einsum(
        "kms,qkse->qmke", isdf_coeffs, partners, preferred_element_type=jnp.float32
    )
    width = densities.shape[1]
    densities = densities.astype(jnp.bfloat16).reshape(2, width, k_local * vectors)
    slabs = jnp.take(w_screen, qsel, axis=0)
    partials = jnp.einsum(
        "qrm,qmx->qrx",
        lax.all_gather(slabs, KA, axis=1, tiled=True),
        densities,
        preferred_element_type=jnp.float32,
    )
    screened = sent_and_summed(partials.astype(jnp.bfloat16), "col", 1)
    screened = screened.astype(jnp.bfloat16).reshape(2, width, k_local, vectors)
    projected = jnp.einsum(
        "kms,qmke->kse", isdf_coeffs, screened, preferred_element_type=jnp.float32
    )
    summed = sent_and_summed(projected.astype(jnp.bfloat16), "col", 1)
    return summed + energies[:, :, None] * amps.astype(jnp.float32)


def solution(mesh):
    torus = Mesh(mesh.devices.reshape(4, 2, 16, mesh.shape["col"]), ("ka_0", "ka_1", "ka_2", "col"))
    placed = (P(KA, "col", None), P(KA, "col", None), P(None, KA, "col"), P(KA, "col"), P(), P())
    return jax.shard_map(
        body, mesh=torus, in_specs=placed, out_specs=P(KA, "col", None), check_vma=False
    )
```

profile of v0, /device:TPU:1, one launch (start us, length us, event | category | flops | bytes accessed | tf_op | source)
XLA Modules:
  0.0 428.2 jit_solution(16825926341223506665)
XLA Ops:
  6.5 6.3 %all-gather = bf16[4,64,192]{2,1,0:T(8,128)(2,1)S(1)} all-gather(bf16[2,64,192]{2,1,0:T(8,128)(2,1)} %param.6), channel_id=2, replica_groups=mesh['ka_0'=4,'ka_1'=2,'ka_2'=16,'col'=4] {'ka_1'}, dimensions={0}, use_global_device_ids=true | all-gather | bytes 147456 | tf_op jit(solution)/shard_map/all_gather | solution.py:19
  12.8 11.5 %all_gather.14 = bf16[8,2,64,192]{3,2,1,0:T(8,128)(2,1)} all-gather(bf16[2,2,64,192]{3,2,1,0:T(8,128)(2,1)S(1)} %bitcast.44), channel_id=1, replica_groups=mesh['ka_0'=4,'ka_1'=2,'ka_2'=16,'col'=4] {'ka_0'}, dimensions={0}, use_global_device_ids=true | all-gather | bytes 491520 | tf_op jit(solution)/shard_map/all_gather | solution.py:19
  24.4 0.7 compare_select_fusion.4
  25.1 1.5 gather_fusion
  26.6 0.7 compare_and_fusion.2
  27.2 0.7 broadcast_select_fusion.1
  27.9 0.8 copy.48
  28.8 0.6 gather_fusion.1
  29.7 108.4 %all-gather.6.cloned.1.call-done = bf16[128,2,64,192]{3,2,1,0:T(8,128)(2,1)} async-done(((bf16[8,2,64,192]{3,2,1,0:T(8,128)(2,1)}), bf16[128,2,64,192]{3,2,1,0:T(8,128)(2,1)}) %all-gather.6.cloned.1.call-update) | async-done | bytes 6291472 | tf_op jit(solution)/shard_map/all_gather | solution.py:19
  138.1 8.3 %copy.50 = bf16[4,2,16,2,64,192]{5,4,3,2,1,0:T(8,128)(2,1)} copy(bf16[4,2,16,2,64,192]{5,4,3,1,0,2:T(8,128)(2,1)} %bitcast.37) | data formatting | bytes 12582912 | tf_op jit(solution)/shard_map/transpose | solution.py:23
  146.4 3.9 gather_fusion.2
  150.5 11.2 %all_to_all.15 = bf16[4,4,64,192]{3,2,1,0:T(8,128)(2,1)S(1)} all-to-all(bf16[4,4,64,192]{3,2,1,0:T(8,128)(2,1)S(1)} %broadcast_in_dim.45), channel_id=1, replica_groups=mesh['ka_0'=4,'ka_1'=2,'ka_2'=16,'col'=4] {'col'}, dimensions={0} | all-to-all | bytes 786432 | tf_op jit(solution)/shard_map/all_to_all | solution.py:32
  161.8 0.5 fusion
  162.3 192.0 %all-gather.4.cloned.1.call-done = bf16[2,2048,512]{2,1,0:T(8,128)(2,1)} async-done(((bf16[2,16,512]{2,1,0:T(8,128)(2,1)}), bf16[2,2048,512]{2,1,0:T(8,128)(2,1)}) %all-gather.4.cloned.1.call-update) | async-done | bytes 4194320 | tf_op jit(solution)/shard_map/all_gather | solution.py:71
  354.3 4.5 %convolution_convert_fusion = bf16[2,2048,384]{2,1,0:T(8,128)(2,1)S(1)} fusion(bf16[2,2048,512]{2,1,0:T(8,128)(2,1)} %all-gather.4.cloned.1.call-done, bf16[2,512,384]{1,2,0:T(8,128)(2,1)S(1)} %bitcast.43), kind=kOutput, calls=%fused_computation.3 | convolution fusion | flops 1612185600 | bytes 8126464 | tf_op jit(solution)/shard_map/qrm,qmx->qrx/dot_general | solution.py:69
  358.8 0.3 copy.67
  359.2 49.6 %all_to_all.16 = bf16[4,2,512,384]{3,2,1,0:T(8,128)(2,1)} all-to-all(bf16[4,2,512,384]{3,2,1,0:T(8,128)(2,1)S(1)} %bitcast.35), channel_id=1, replica_groups=mesh['ka_0'=4,'ka_1'=2,'ka_2'=16,'col'=4] {'col'}, dimensions={0} | all-to-all | bytes 6291456 | tf_op jit(solution)/shard_map/all_to_all | solution.py:49
  408.7 2.7 reduce_sum.32
  411.4 0.1 convert_reduce_fusion
  411.5 0.2 copy.57
  411.7 0.3 fusion.1
  412.0 0.1 copy.58
  412.2 8.4 %all_to_all.17 = bf16[4,2,64,192]{3,2,1,0:T(8,128)(2,1)S(1)} all-to-all(bf16[4,2,64,192]{3,2,1,0:T(8,128)(2,1)S(1)} %copy.59), channel_id=1, replica_groups=mesh['ka_0'=4,'ka_1'=2,'ka_2'=16,'col'=4] {'col'}, dimensions={0} | all-to-all | bytes 393216 | tf_op jit(solution)/shard_map/all_to_all | solution.py:49
  420.6 0.7 multiply_add_fusion
  (27 shorter events, 0.7 us)
Async XLA Ops:
  6.5 155.2 %copy-start = (bf16[2,512,256]{2,1,0:T(8,128)(2,1)S(1)}, bf16[2,512,256]{2,1,0:T(8,128)(2,1)}, u32[]{:S(2)}) copy-start(bf16[2,512,256]{2,1,0:T(8,128)(2,1)} %param.7) | copy-start | bytes 1572868
  6.5 131.6 %all-gather.6.cloned.1.call-start = ((), (), s32[]{:S(2)}) async-start(), calls=%async_computation.4 | async-start | bytes 8912896 | tf_op jit(solution)/shard_map/all_gather | solution.py:19
  24.3 329.9 %all-gather.4.cloned.1.call-start = ((), (), s32[]{:S(2)}) async-start(), calls=%async_computation.3 | async-start | bytes 4227072 | tf_op jit(solution)/shard_map/all_gather | solution.py:71
  408.7 11.9 %copy-start.1 = (bf16[2,64,192]{2,1,0:T(8,128)(2,1)S(1)}, bf16[2,64,192]{2,1,0:T(8,128)(2,1)}, u32[]{:S(2)}) copy-start(bf16[2,64,192]{2,1,0:T(8,128)(2,1)} %param.6) | copy-start | bytes 147460
  408.7 11.9 %copy-start.2 = (f32[2,64]{1,0:T(2,128)S(1)}, f32[2,64]{1,0:T(2,128)}, u32[]{:S(2)}) copy-start(f32[2,64]{1,0:T(2,128)} %param.9) | copy-start | bytes 1540
Sparse Core Ops, SparseCore 0:
  24.5 113.6 all-gather.5
  142.5 211.6 all-gather.3
where the time goes:
time: 429 us; the launch traced here: 428 us
  waiting for transfers between devices  300 us (70%)
  blocking collectives  87 us (20%)
  local copies, waits for them, and re-layouts  16.1 us (4%)
  between operations  13.6 us (3%)
  other arithmetic  5.77 us (1%)
  matrix products  5.3 us (1%)
    all_gather x1, waiting for transfers between devices, body(): lax.all_gather(slabs, KA, axis=1, tiled=True)  192 us
    all_gather x1, waiting for transfers between devices, gather_in_order(): pieces = lax.all_gather(pieces, axes[k], axis=0, tiled=True)  108 us
    all_to_all x2, blocking collectives, sent_and_summed(): lax.all_to_all(pieces, axis, split_axis=0, concat_axis=0, tiled=True)  58 us
    all_gather x2, blocking collectives, gather_in_order(): pieces = lax.all_gather(pieces, axes[k], axis=0, tiled=True)  17.8 us
    all_to_all x1, blocking collectives, sent_to_all(): lax.all_to_all(jnp.broadcast_to(array[None], (length, *array.shape)), axi...  11.2 us
  transfers between devices with their start and end apart: 2, of which 2 were waited for; matrix products, arithmetic and copies ran while one was open for 4% of the time, Pallas kernels for 0%

commit v1 on v0

--- a/solution.py
+++ b/solution.py
@@ -16,7 +16,8 @@
 def gather_in_order(array, axes, order):
     pieces = array[None]
     for k in order:
-        pieces = lax.all_gather(pieces, axes[k], axis=0, tiled=True)
+        repeated = jnp.stack([pieces] * lax.axis_size(axes[k]))
+        pieces = jnp.concatenate(lax.all_to_all(repeated, axes[k], 0, 0), axis=0)
     carried = [lax.axis_size(axes[k]) for k in reversed(order)]
     pieces = pieces.reshape(*carried, *array.shape)
     turned = sorted(range(len(order)), key=lambda place: order[len(order) - 1 - place])

time: 429 us -> 523 us (1.22)
  waiting for transfers between devices: 300 us -> 382 us
  starting transfers between devices: 0.04 us -> 15.1 us
  blocking collectives: 87 us -> 80.6 us
    all_to_all x0 -> x1, waiting for transfers between devices: none -> 382 us  [gather_in_order(): pieces = jnp.concatenate(lax.all_to_all(repeated, axes[k], 0, 0), axis=0)]
    all_gather x1, waiting for transfers between devices: 192 us -> 0.02 us  [body(): lax.all_gather(slabs, KA, axis=1, tiled=True)]
    all_gather x1 -> x0, waiting for transfers between devices: 108 us -> none  [gather_in_order(): pieces = lax.all_gather(pieces, axes[k], axis=0, tiled=True)]
    all_to_all x0 -> x2, blocking collectives: none -> 20.4 us  [gather_in_order(): pieces = jnp.concatenate(lax.all_to_all(repeated, axes[k], 0, 0), axis=0)]
    all_gather x2 -> x0, blocking collectives: 17.8 us -> none  [gather_in_order(): pieces = lax.all_gather(pieces, axes[k], axis=0, tiled=True)]
    all_to_all x0 -> x1, starting transfers between devices: none -> 15.1 us  [gather_in_order(): pieces = jnp.concatenate(lax.all_to_all(repeated, axes[k], 0, 0), axis=0)]
    another operation x0 -> x3, local copies, waits for them, and re-layouts: none -> 12.6 us  [the longest x1 8.26 us: gather_in_order(): pieces = pieces.reshape(*carried, *array.shape)]
    all_to_all x2, blocking collectives: 58 us -> 48.6 us  [sent_and_summed(): lax.all_to_all(pieces, axis, split_axis=0, concat_axis=0, tiled=True)]
  transfers between devices with their start and end apart: 2 -> 2, of which waited for: 2 -> 1; matrix products, arithmetic and copies ran while one was open for 4% -> 3% of each run, Pallas kernels for 0% -> 0%
where the time goes in v1:
time: 523 us; the launch traced here: 522 us
  waiting for transfers between devices  382 us (73%)
  blocking collectives  80.6 us (15%)
  local copies, waits for them, and re-layouts  19.8 us (4%)
  starting transfers between devices  15.1 us (3%)
  between operations  13.6 us (3%)
  other arithmetic  5.41 us (1%)
  matrix products  5.3 us (1%)
    all_to_all x1, waiting for transfers between devices, gather_in_order(): pieces = jnp.concatenate(lax.all_to_all(repeated, axes[k], 0, 0), axis=0)  382 us
    all_to_all x2, blocking collectives, sent_and_summed(): lax.all_to_all(pieces, axis, split_axis=0, concat_axis=0, tiled=True)  48.6 us
    all_to_all x2, blocking collectives, gather_in_order(): pieces = jnp.concatenate(lax.all_to_all(repeated, axes[k], 0, 0), axis=0)  20.4 us
    all_to_all x1, starting transfers between devices, gather_in_order(): pieces = jnp.concatenate(lax.all_to_all(repeated, axes[k], 0, 0), axis=0)  15.1 us
    all_to_all x1, blocking collectives, sent_to_all(): lax.all_to_all(jnp.broadcast_to(array[None], (length, *array.shape)), axi...  11.6 us
  transfers between devices with their start and end apart: 2, of which 1 were waited for; matrix products, arithmetic and copies ran while one was open for 3% of the time, Pallas kernels for 0%

profile of v1, /device:TPU:1, one launch (start us, length us, event | category | flops | bytes accessed | tf_op | source)
XLA Modules:
  0.0 522.1 jit_solution(14933848081847449666)
XLA Ops:
  6.5 1.0 pad_maximum_fusion
  7.5 9.5 %all_to_all.30 = bf16[2,1,2,64,192]{4,3,2,1,0:T(8,128)(2,1)S(1)} all-to-all(bf16[2,1,2,64,192]{4,3,2,1,0:T(8,128)(2,1)S(1)} %pad_maximum_fusion), channel_id=1, replica_groups=mesh['ka_0'=4,'ka_1'=2,'ka_2'=16,'col'=4] {'ka_1'}, dimensions={0} | all-to-all | bytes 196608 | tf_op jit(solution)/shard_map/all_to_all | solution.py:20
  17.0 10.9 %all_to_all.31 = bf16[4,2,2,64,192]{4,3,2,1,0:T(8,128)(2,1)S(1)} all-to-all(bf16[4,2,2,64,192]{4,3,2,1,0:T(8,128)(2,1)S(1)} %stack.10), channel_id=1, replica_groups=mesh['ka_0'=4,'ka_1'=2,'ka_2'=16,'col'=4] {'ka_0'}, dimensions={0} | all-to-all | bytes 786432 | tf_op jit(solution)/shard_map/all_to_all | solution.py:20
  27.9 4.3 stack.11
  32.2 15.1 %all-to-all-start.2 = ((bf16[16,8,2,64,192]{4,3,2,1,0:T(8,128)(2,1)}), bf16[16,8,2,64,192]{4,3,2,1,0:T(8,128)(2,1)}, u32[]{:S(2)}, u32[]{:S(2)}) async-start(bf16[16,8,2,64,192]{4,3,2,1,0:T(8,128)(2,1)} %stack.11), calls=%async_computation.2 | async-start | bytes 16777216 | tf_op jit(solution)/shard_map/all_to_all | solution.py:20
  47.4 1.5 gather_fusion
  48.9 0.7 broadcast_select_fusion.1
  49.7 0.1 copy.40
  49.8 0.6 gather_fusion.1
  50.8 382.2 %all-to-all-done.2 = bf16[16,8,2,64,192]{4,3,2,1,0:T(8,128)(2,1)} async-done(((bf16[16,8,2,64,192]{4,3,2,1,0:T(8,128)(2,1)}), bf16[16,8,2,64,192]{4,3,2,1,0:T(8,128)(2,1)}, u32[]{:S(2)}, u32[]{:S(2)}) %all-to-all-start.2) | async-done | bytes 6291488 | tf_op jit(solution)/shard_map/all_to_all | solution.py:20
  433.0 8.3 %copy.42 = bf16[16,4,2,2,64,192]{5,4,3,0,2,1:T(8,128)(2,1)} copy(bf16[16,4,2,2,64,192]{5,4,3,2,1,0:T(8,128)(2,1)} %bitcast.5) | data formatting | bytes 12582912 | tf_op jit(solution)/shard_map/reshape;reshape | solution.py:22
  441.2 3.9 gather_fusion.2
  445.3 11.6 %all_to_all.32 = bf16[4,4,64,192]{3,2,1,0:T(8,128)(2,1)S(1)} all-to-all(bf16[4,4,64,192]{3,2,1,0:T(8,128)(2,1)S(1)} %broadcast_in_dim.41), channel_id=1, replica_groups=mesh['ka_0'=4,'ka_1'=2,'ka_2'=16,'col'=4] {'col'}, dimensions={0} | all-to-all | bytes 786432 | tf_op jit(solution)/shard_map/all_to_all | solution.py:33
  456.9 0.5 fusion
  457.5 4.5 convolution_convert_fusion
  462.1 0.3 copy.59
  462.4 40.2 %all_to_all.33 = bf16[4,2,512,384]{3,2,1,0:T(8,128)(2,1)} all-to-all(bf16[4,2,512,384]{3,2,1,0:T(8,128)(2,1)S(1)} %bitcast.37), channel_id=1, replica_groups=mesh['ka_0'=4,'ka_1'=2,'ka_2'=16,'col'=4] {'col'}, dimensions={0} | all-to-all | bytes 6291456 | tf_op jit(solution)/shard_map/all_to_all | solution.py:50
  502.6 2.7 reduce_sum.32
  505.3 0.1 convert_reduce_fusion
  505.4 0.2 copy.49
  505.6 0.3 fusion.1
  505.9 0.1 copy.50
  506.0 8.4 %all_to_all.34 = bf16[4,2,64,192]{3,2,1,0:T(8,128)(2,1)S(1)} all-to-all(bf16[4,2,64,192]{3,2,1,0:T(8,128)(2,1)S(1)} %copy.51), channel_id=1, replica_groups=mesh['ka_0'=4,'ka_1'=2,'ka_2'=16,'col'=4] {'col'}, dimensions={0} | all-to-all | bytes 393216 | tf_op jit(solution)/shard_map/all_to_all | solution.py:50
  514.5 0.7 multiply_add_fusion
  (33 shorter events, 0.8 us)
Async XLA Ops:
  6.5 450.4 %copy-start = (bf16[2,512,256]{2,1,0:T(8,128)(2,1)S(1)}, bf16[2,512,256]{2,1,0:T(8,128)(2,1)}, u32[]{:S(2)}) copy-start(bf16[2,512,256]{2,1,0:T(8,128)(2,1)} %param.7) | copy-start | bytes 1572868
  32.2 15.2 %copy-start.4 = (s32[2]{0:T(128)S(1)}, s32[2]{0:T(128)}, u32[]{:S(2)}) copy-start(s32[2]{0:T(128)} %param.10) | copy-start | bytes 28
  32.2 17.4 %copy-start.2 = (s32[2,256]{1,0:T(2,128)S(1)}, s32[2,256]{1,0:T(2,128)}, u32[]{:S(2)}) copy-start(s32[2,256]{1,0:T(2,128)} %param.11) | copy-start | bytes 6148
  32.2 400.7 %all-to-all-start.2 = ((bf16[16,8,2,64,192]{4,3,2,1,0:T(8,128)(2,1)}), bf16[16,8,2,64,192]{4,3,2,1,0:T(8,128)(2,1)}, u32[]{:S(2)}, u32[]{:S(2)}) async-start(bf16[16,8,2,64,192]{4,3,2,1,0:T(8,128)(2,1)} %stack.11), calls=%async_computation.2 | async-start | bytes 16777216 | tf_op jit(solution)/shard_map/all_to_all | solution.py:20
  47.3 410.2 %all-gather.2.cloned.1.call-start = ((), (), s32[]{:S(2)}) async-start(), calls=%async_computation.6 | async-start | bytes 4227072 | tf_op jit(solution)/shard_map/all_gather | solution.py:72
  502.6 11.9 %copy-start.1 = (bf16[2,64,192]{2,1,0:T(8,128)(2,1)S(1)}, bf16[2,64,192]{2,1,0:T(8,128)(2,1)}, u32[]{:S(2)}) copy-start(bf16[2,64,192]{2,1,0:T(8,128)(2,1)} %param.6) | copy-start | bytes 147460
  502.6 11.9 %copy-start.3 = (f32[2,64]{1,0:T(2,128)S(1)}, f32[2,64]{1,0:T(2,128)}, u32[]{:S(2)}) copy-start(f32[2,64]{1,0:T(2,128)} %param.9) | copy-start | bytes 1540
Sparse Core Ops, SparseCore 0:
  52.5 363.6 all-gather.1
